TPU v7x, 32 devices: a whole 2x2x4 slice. The times are simulated.
32 devices in a mesh: seq: 8 (over y, x, core), mp: 4 (over z).
Axes of the slice: x: 2, y: 2, z: 4, core: 2. Of those that a mesh axis runs over, the one named last changes fastest.
Arguments:
- inputs: bfloat16 [8192, 4096], P('seq', 'mp'), may hold values from -6 to 6
- conv_weight: bfloat16 [4, 4096], P(None, 'mp'), may hold values from -3 to 3
- conv_bias: bfloat16 [4096], P('mp'), may hold values from -3 to 3
- doc_start: int32 [8192], P('seq'), may hold values from 0 to 8191, as said below
- counts: int32 [8], P('seq'), may hold values from 341 to 1024
Outputs:
- gram: float32 [4096, 4096], P('seq', 'mp')
Inputs may be any that keep to these rules, and one draw needn't show every extreme that they name: doc_start is never above the token's own position, and for t > 0 either doc_start[t] == t or doc_start[t] == doc_start[t - 1]; doc_start[0] is 0.
All inputs are finite; a program needn't handle non-finite values.
Results may differ from a plain program's by a relative error of at most 0.0003.
Values may be sent and summed in bfloat16 or wider, within the bound.
A program may use at most 64 MiB of HBM per device.

v0:
```python
import jax
import jax.numpy as jnp
from jax import lax
from jax.sharding import PartitionSpec as P


def passed_along(x, axis, by):
    peers = lax.axis_size(axis)
    pairs = [(i, i + by) for i in range(peers) if 0 <= i + by < peers]
    return lax.ppermute(x, axis, pairs)


def causal_conv(extended, weights, bias, position, doc_start, length):
    kernel_len = weights.shape[0]
    summed = jnp.zeros((length, weights.shape[1]), jnp.float32) + bias.astype(jnp.float32)
    for lag in range(kernel_len):
        window = extended[kernel_len - 1 - lag : kernel_len - 1 - lag + length].astype(jnp.float32)
        usable = position - lag >= doc_start
        summed = summed + jnp.where(usable[:, None], weights[lag].astype(jnp.float32) * window, 0.0)
    return jax.nn.silu(summed).astype(jnp.bfloat16)


def on_device(inputs, conv_weight, conv_bias, doc_start, counts):
    row_count = inputs.shape[0]
    kernel_len = conv_weight.shape[0]
    position = lax.axis_index("seq") * row_count + jnp.arange(row_count, dtype=jnp.int32)
    counted = jnp.arange(row_count, dtype=jnp.int32) < counts[0]
    token_total = lax.psum(counts.astype(jnp.float32)[0], "seq")
    prior = passed_along(inputs[row_count - (kernel_len - 1) :], "seq", 1)
    extended = jnp.concatenate([prior, inputs], axis=0)
    own_feats = causal_conv(extended, conv_weight, conv_bias, position, doc_start, row_count)
    kept = jnp.where(counted[:, None], own_feats, jnp.zeros_like(own_feats))
    whole = lax.all_gather(own_feats, "mp", axis=1, tiled=True)
    summed = lax.psum_scatter(
        lax.dot_general(whole, kept, (((0,), (0,)), ((), ())), preferred_element_type=jnp.float32),
        "seq",
        scatter_dimension=0,
        tiled=True,
    )
    return summed / token_total


def solution(mesh):
    placed = (P("seq", "mp"), P(None, "mp"), P("mp"), P("seq"), P("seq"))
    return jax.shard_map(
        on_device, mesh=mesh, in_specs=placed, out_specs=P("seq", "mp"), check_vma=False
    )
```

profile of v0, /device:TPU:0, one launch (start us, length us, event | category | flops | bytes accessed | tf_op | source)
XLA Modules:
  0.0 316.0 jit_solution(3767885994745322081)
XLA Ops:
  6.5 0.0 all-gather.2.cloned.1.call-start
  6.5 0.7 slice.26
  7.3 2.4 collective-permute-start
  9.7 0.9 slice_convert_fusion.3
  10.5 0.7 fusion.6
  11.2 0.7 convert_element_type.29
  11.9 0.0 collective-permute-done
  11.9 9.8 %multiply_convert_fusion = bf16[1024,1024]{1,0:T(8,128)(2,1)} fusion(bf16[1024,1024]{1,0:T(8,128)(2,1)} %param.5, bf16[3,1024]{1,0:T(4,128)(2,1)S(1)} %collective-permute-done, f32[1024]{0:T(1024)S(1)} %bitcast.10, f32[1024]{0:T(1024)S(1)} %bitcast.11, f32[1024]{0:T(1024)S(1)} %bitcast.9, f32[1024]{0:T(1024)S(1)} %bitcast.8, f32[1024]{0:T(1024)S(1)} %convert_element_type.29, ...), kind=kLoop, calls=%fused_computation | loop fusion | flops 31457280 | bytes 4225024 | tf_op jit(solution)/shard_map/convert_element_type | solution.py:20
  21.7 0.0 all-gather.2.cloned.1.call-update
  21.7 0.0 reduce-scatter.2.cloned.1.call-start
  22.4 152.1 %all-gather.2.cloned.1.call-done = bf16[1024,4096]{1,0:T(8,128)(2,1)} async-done(((bf16[1024,1024]{1,0:T(8,128)(2,1)}), bf16[1024,4096]{1,0:T(8,128)(2,1)}) %all-gather.2.cloned.1.call-update) | async-done | bytes 8388624 | tf_op jit(solution)/shard_map/all_gather | solution.py:33
  174.5 16.3 %fusion.2 = f32[4096,1024]{1,0:T(8,128)} fusion(bf16[1024,4096]{1,0:T(8,128)(2,1)} %all-gather.2.cloned.1.call-done, bf16[1024,1024]{1,0:T(8,128)(2,1)} %multiply_convert_fusion, pred[1024]{0:T(1024)(128)(4,1)S(1)} %iota_compare_fusion), kind=kOutput, calls=%fused_computation.6 | convolution fusion | flops 8590983168 | bytes 27264000 | tf_op jit(solution)/shard_map/dot_general | solution.py:35
  190.8 0.0 reduce-scatter.2.cloned.1.call-update
  190.9 15.0 %psum.7 = f32[]{:T(128)} all-reduce(f32[]{:T(128)} %bitcast.5), channel_id=1, replica_groups=mesh['seq'=8,'mp'=4] {'seq'}, use_global_device_ids=true, to_apply=%region_1.2 | all-reduce | flops 1 | bytes 8 | tf_op jit(solution)/shard_map/psum | solution.py:28
  205.8 99.5 %reduce-scatter.2.cloned.1.call-done = f32[512,1024]{1,0:T(8,128)} async-done(((f32[4096,1024]{1,0:T(8,128)}), f32[512,1024]{1,0:T(8,128)}) %reduce-scatter.2.cloned.1.call-update) | async-done | bytes 2097168 | tf_op jit(solution)/shard_map/reduce_scatter | solution.py:34
  305.4 3.8 %broadcast_divide_fusion = f32[512,1024]{1,0:T(8,128)} fusion(f32[512,1024]{1,0:T(8,128)} %reduce-scatter.2.cloned.1.call-done, f32[]{:T(128)} %psum.7), kind=kLoop, calls=%fused_computation.9 | loop fusion | flops 524288 | bytes 4194308 | tf_op jit(solution)/shard_map/div | solution.py:40
  (1 shorter events, 0.0 us)
Async XLA Ops:
  6.5 168.0 %all-gather.2.cloned.1.call-start = ((), (), s32[]{:S(2)}) async-start(), calls=%async_computation.1 | async-start | bytes 10485760 | tf_op jit(solution)/shard_map/all_gather | solution.py:33
  7.3 4.7 %collective-permute-start = (bf16[3,1024]{1,0:T(4,128)(2,1)S(1)}, bf16[3,1024]{1,0:T(4,128)(2,1)S(1)}, u32[]{:S(2)}, u32[]{:S(2)}) collective-permute-start(bf16[3,1024]{1,0:T(4,128)(2,1)S(1)} %slice.26), channel_id=1, source_target_pairs={{0,4},{4,8},{8,12},{12,16},{16,20},{20,24},{24,28},{1,5},{5,9},{9,... | collective-permute-start | bytes 18440 | tf_op jit(solution)/shard_map/ppermute | solution.py:10
  21.7 283.7 %reduce-scatter.2.cloned.1.call-start = ((), (), s32[]{:S(2)}) async-start(), calls=%async_computation.2 | async-start | bytes 18874368 | tf_op jit(solution)/shard_map/reduce_scatter | solution.py:34
Sparse Core Ops, SparseCore 0:
  21.8 152.6 all-gather.1
  191.0 114.3 reduce-scatter.1
where the time goes:
time: 316 us
  waiting for transfers between devices  252 us (80%)
  matrix products  16.3 us (5%)
  other arithmetic  15.9 us (5%)
  blocking collectives  15 us (5%)
  between operations  14.1 us (4%)
    all_gather x1, waiting for transfers between devices, on_device(): whole = lax.all_gather(own_feats, 'mp', axis=1, tiled=True)  152 us
    reduce_scatter x1, waiting for transfers between devices, on_device(): lax.psum_scatter(lax.dot_general(whole, kept, (((0,), (0,)), ((), ())), p...  99.5 us
    dot_general x1, matrix products, on_device(): lax.dot_general(whole, kept, (((0,), (0,)), ((), ())), preferred_element_...  16.3 us
    psum x1, blocking collectives, on_device(): token_total = lax.psum(counts.astype(jnp.float32)[0], 'seq')  15 us
    convert_element_type x1, other arithmetic, causal_conv(): return jax.nn.silu(summed).astype(jnp.bfloat16)  9.78 us
  transfers between devices with their start and end apart: 3, of which 2 were waited for; matrix products, arithmetic and copies ran while one was open for 1% of the time, Pallas kernels for 0%

commit v1 on v0

--- a/solution.py
+++ b/solution.py
@@ -30,7 +30,9 @@
     extended = jnp.concatenate([prior, inputs], axis=0)
     own_feats = causal_conv(extended, conv_weight, conv_bias, position, doc_start, row_count)
     kept = jnp.where(counted[:, None], own_feats, jnp.zeros_like(own_feats))
-    whole = lax.all_gather(own_feats, "mp", axis=1, tiled=True)
+    whole = jnp.concatenate(
+        lax.all_to_all(jnp.stack([own_feats] * lax.axis_size("mp")), "mp", 0, 0), axis=1
+    )
     summed = lax.psum_scatter(
         lax.dot_general(whole, kept, (((0,), (0,)), ((), ())), preferred_element_type=jnp.float32),
         "seq",

time: 316 us -> 361 us (1.14)
  waiting for transfers between devices: 252 us -> 286 us
  local copies, waits for them, and re-layouts: 0.72 us -> 7.9 us
  starting transfers between devices: 2.43 us -> 8.21 us
    all_to_all x0 -> x1, waiting for transfers between devices: none -> 183 us  [on_device(): lax.all_to_all(jnp.stack([own_feats] * lax.axis_size('mp')), 'mp', 0, 0)]
    all_gather x1 -> x0, waiting for transfers between devices: 152 us -> none  [on_device(): whole = lax.all_gather(own_feats, 'mp', axis=1, tiled=True)]
    all_to_all x0 -> x1, starting transfers between devices: none -> 5.82 us  [on_device(): lax.all_to_all(jnp.stack([own_feats] * lax.axis_size('mp')), 'mp', 0, 0)]
    another operation x0 -> x1, local copies, waits for them, and re-layouts: none -> 4.32 us  [on_device(): jnp.stack([own_feats] * lax.axis_size('mp'))]
where the time goes in v1:
time: 361 us
  waiting for transfers between devices  286 us (79%)
  other arithmetic  15.9 us (4%)
  matrix products  14.6 us (4%)
  between operations  14.1 us (4%)
  blocking collectives  14 us (4%)
  starting transfers between devices  8.21 us (2%)
  local copies, waits for them, and re-layouts  7.9 us (2%)
    all_to_all x1, waiting for transfers between devices, on_device(): lax.all_to_all(jnp.stack([own_feats] * lax.axis_size('mp')), 'mp', 0, 0)  183 us
    reduce_scatter x1, waiting for transfers between devices, on_device(): lax.psum_scatter(lax.dot_general(whole, kept, (((0,), (0,)), ((), ())), p...  103 us
    dot_general x1, matrix products, on_device(): lax.dot_general(whole, kept, (((0,), (0,)), ((), ())), preferred_element_...  14.6 us
    psum x1, blocking collectives, on_device(): token_total = lax.psum(counts.astype(jnp.float32)[0], 'seq')  14 us
    convert_element_type x1, other arithmetic, causal_conv(): return jax.nn.silu(summed).astype(jnp.bfloat16)  9.83 us
  transfers between devices with their start and end apart: 3, of which 2 were waited for; matrix products, arithmetic and copies ran while one was open for 1% of the time, Pallas kernels for 0%

profile of v1, /device:TPU:0, one launch (start us, length us, event | category | flops | bytes accessed | tf_op | source)
XLA Modules:
  0.0 360.7 jit_solution(5523192051224670768)
XLA Ops:
  6.5 0.7 slice.26
  7.3 2.4 collective-permute-start
  9.7 0.9 slice_convert_fusion.3
  10.5 0.7 fusion.6
  11.2 0.7 convert_element_type.29
  11.9 0.0 collective-permute-done
  11.9 9.8 %multiply_convert_fusion = bf16[1024,1024]{1,0:T(8,128)(2,1)} fusion(bf16[1024,1024]{1,0:T(8,128)(2,1)} %param.5, bf16[3,1024]{1,0:T(4,128)(2,1)S(1)} %collective-permute-done, f32[1024]{0:T(1024)S(1)} %bitcast.13, f32[1024]{0:T(1024)S(1)} %bitcast.14, f32[1024]{0:T(1024)S(1)} %bitcast.12, f32[1024]{0:T(1024)S(1)} %bitcast.11, ...), kind=kLoop, calls=%fused_computation | loop fusion | flops 31457280 | bytes 4225024 | tf_op jit(solution)/shard_map/convert_element_type | solution.py:20
  21.7 2.9 copy.6
  24.6 4.3 %stack.2 = bf16[4,1024,1024]{1,2,0:T(8,128)(2,1)} broadcast(bf16[1024,1024]{0,1:T(8,128)(2,1)S(1)} %copy.6), dimensions={1,2} | broadcast | bytes 10485760 | tf_op jit(solution)/shard_map/stack | solution.py:34
  28.9 0.0 copy-start
  28.9 5.8 %all-to-all-start = ((bf16[4,1024,1024]{1,2,0:T(8,128)(2,1)}), bf16[4,1024,1024]{1,2,0:T(8,128)(2,1)}, u32[]{:S(2)}, u32[]{:S(2)}) async-start(bf16[4,1024,1024]{1,2,0:T(8,128)(2,1)} %stack.2), calls=%async_computation | async-start | bytes 16777216 | tf_op jit(solution)/shard_map/all_to_all | solution.py:34
  34.7 0.0 reduce-scatter.2.cloned.1.call-start
  35.4 183.1 %all-to-all-done = bf16[4,1024,1024]{1,2,0:T(8,128)(2,1)} async-done(((bf16[4,1024,1024]{1,2,0:T(8,128)(2,1)}), bf16[4,1024,1024]{1,2,0:T(8,128)(2,1)}, u32[]{:S(2)}, u32[]{:S(2)}) %all-to-all-start) | async-done | bytes 8388640 | tf_op jit(solution)/shard_map/all_to_all | solution.py:34
  218.5 0.0 copy-done
  218.5 14.6 %fusion.2 = f32[4096,1024]{1,0:T(8,128)} fusion(bf16[1024,4096]{0,1:T(8,128)(2,1)} %bitcast.5, bf16[1024,1024]{1,0:T(8,128)(2,1)S(1)} %copy-done, pred[1024]{0:T(1024)(128)(4,1)S(1)} %iota_compare_fusion), kind=kOutput, calls=%fused_computation.6 | convolution fusion | flops 8590983168 | bytes 27264000 | tf_op jit(solution)/shard_map/dot_general | solution.py:37
  233.2 0.0 reduce-scatter.2.cloned.1.call-update
  233.2 14.0 %psum.7 = f32[]{:T(128)} all-reduce(f32[]{:T(128)} %bitcast.7), channel_id=1, replica_groups=mesh['seq'=8,'mp'=4] {'seq'}, use_global_device_ids=true, to_apply=%region_1.2 | all-reduce | flops 1 | bytes 8 | tf_op jit(solution)/shard_map/psum | solution.py:28
  247.2 102.8 %reduce-scatter.2.cloned.1.call-done = f32[512,1024]{1,0:T(8,128)} async-done(((f32[4096,1024]{1,0:T(8,128)}), f32[512,1024]{1,0:T(8,128)}) %reduce-scatter.2.cloned.1.call-update) | async-done | bytes 2097168 | tf_op jit(solution)/shard_map/reduce_scatter | solution.py:36
  350.0 3.8 %broadcast_divide_fusion = f32[512,1024]{1,0:T(8,128)} fusion(f32[512,1024]{1,0:T(8,128)} %reduce-scatter.2.cloned.1.call-done, f32[]{:T(128)} %psum.7), kind=kLoop, calls=%fused_computation.9 | loop fusion | flops 524288 | bytes 4194308 | tf_op jit(solution)/shard_map/div | solution.py:42
  (1 shorter events, 0.0 us)
Async XLA Ops:
  7.3 4.7 %collective-permute-start = (bf16[3,1024]{1,0:T(4,128)(2,1)S(1)}, bf16[3,1024]{1,0:T(4,128)(2,1)S(1)}, u32[]{:S(2)}, u32[]{:S(2)}) collective-permute-start(bf16[3,1024]{1,0:T(4,128)(2,1)S(1)} %slice.26), channel_id=1, source_target_pairs={{0,4},{4,8},{8,12},{12,16},{16,20},{20,24},{24,28},{1,5},{5,9},{9,... | collective-permute-start | bytes 18440 | tf_op jit(solution)/shard_map/ppermute | solution.py:10
  28.9 189.6 %copy-start = (bf16[1024,1024]{1,0:T(8,128)(2,1)S(1)}, bf16[1024,1024]{1,0:T(8,128)(2,1)}, u32[]{:S(2)}) copy-start(bf16[1024,1024]{1,0:T(8,128)(2,1)} %multiply_convert_fusion) | copy-start | bytes 6291460
  28.9 189.6 %all-to-all-start = ((bf16[4,1024,1024]{1,2,0:T(8,128)(2,1)}), bf16[4,1024,1024]{1,2,0:T(8,128)(2,1)}, u32[]{:S(2)}, u32[]{:S(2)}) async-start(bf16[4,1024,1024]{1,2,0:T(8,128)(2,1)} %stack.2), calls=%async_computation | async-start | bytes 16777216 | tf_op jit(solution)/shard_map/all_to_all | solution.py:34
  34.7 315.3 %reduce-scatter.2.cloned.1.call-start = ((), (), s32[]{:S(2)}) async-start(), calls=%async_computation.2 | async-start | bytes 18874368 | tf_op jit(solution)/shard_map/reduce_scatter | solution.py:36
Sparse Core Ops, SparseCore 0:
  233.3 116.6 reduce-scatter.1
